TPU v7x, 32 devices: a whole 2x2x4 slice. The times are simulated.
32 devices in a mesh: ep: 8 (over z, y), tp: 4 (over x, core).
Axes of the slice: x: 2, y: 2, z: 4, core: 2. Of those that a mesh axis runs over, the one named last changes fastest.
Arguments:
- tokens: bfloat16 [4096, 2048], P(('ep', 'tp')), may hold values from -6 to 6
- norm_gain: float32 [2048], replicated, may hold values from 0.1 to 1.9
- expert_ids: int32 [4096, 6], P(('ep', 'tp')), may hold values from 0 to 15, as said below
- slot_index: int32 [4096, 6], P(('ep', 'tp')), may hold values from 0 to 63, as said below
- dropped: int32 [4096, 6], P(('ep', 'tp')), may hold values from 0 to 1, as said below
- gates: float32 [4096, 6], P(('ep', 'tp')), may hold values from 0.05 to 0.8
- w_gate: bfloat16 [16, 2048, 704], P('ep', None, 'tp'), may hold values from -0.125 to 0.125
- w_up: bfloat16 [16, 2048, 704], P('ep', None, 'tp'), may hold values from -0.125 to 0.125
- w_down: bfloat16 [16, 2048, 704], P('ep', None, 'tp'), may hold values from -0.21875 to 0.21875
- shared_gate: bfloat16 [2048, 1408], P(None, 'tp'), may hold values from -0.125 to 0.125
- shared_up: bfloat16 [2048, 1408], P(None, 'tp'), may hold values from -0.125 to 0.125
- shared_down: bfloat16 [1408, 2048], replicated, may hold values from -0.15625 to 0.15625
Outputs:
- layer_out: bfloat16 [4096, 2048], P(('ep', 'tp'))
Inputs may be any that keep to these rules, and one draw needn't show every extreme that they name: `expert_ids`: each token names 6 different experts; some expert has 64 kept pairs from the tokens of every device. `slot_index`: for a kept pair, its place among the slots of its expert for the tokens of its device (the tokens n with one value of n // 128); the kept pairs of one device and one expert have distinct places; 0 for a dropped pair. `dropped`: 1 for the pairs of a device and an expert beyond the 64 that are kept.
All inputs are finite; a program needn't handle non-finite values.
Results may differ from a plain program's by a relative error of at most 0.0054.
Values may be sent and summed in bfloat16 or wider, within the bound.
A program may use at most 128 MiB of HBM per device.

v0:
```python
import jax
import jax.numpy as jnp
from jax import lax
from jax.sharding import PartitionSpec as P

TOP = 6
EXP_DEV = 2
TOK_DEV = 128
norm_eps = 1e-06


def swiglu(left, right):
    return jax.nn.silu(left) * right


def on_device(
    tokens,
    norm_gain,
    expert_ids,
    slot_index,
    dropped,
    gates,
    w_gate,
    w_up,
    w_down,
    shared_gate,
    shared_up,
    shared_down,
):
    n_expert_groups = lax.axis_size("ep")
    experts = EXP_DEV * n_expert_groups
    capacity = TOK_DEV * TOP * 4 // (experts * 3)
    model_width = tokens.shape[1]
    local_rows = tokens.shape[0]
    values = tokens.astype(jnp.float32)
    scale = lax.rsqrt(jnp.mean(values * values, axis=-1, keepdims=True) + norm_eps)
    normed = (values * scale * norm_gain).astype(jnp.bfloat16)
    destination_position = expert_ids * capacity + slot_index
    kept_pair = dropped == 0
    matrix_breadth = lax.iota(jnp.int32, experts * capacity)
    matches = (destination_position[:, :, None] == matrix_breadth[None, None, :]) & kept_pair[
        :, :, None
    ]
    dispatch_table = jnp.any(matches, axis=1).astype(jnp.bfloat16)
    outgoing = lax.dot_general(
        dispatch_table, normed, (((0,), (0,)), ((), ())), preferred_element_type=jnp.float32
    ).astype(jnp.bfloat16)
    boxes = outgoing.reshape(n_expert_groups, EXP_DEV, capacity, model_width)
    received = lax.all_to_all(boxes, "ep", split_axis=0, concat_axis=0, tiled=True)
    gate_all = lax.all_gather(w_gate, "tp", axis=2, tiled=True)
    up_all = lax.all_gather(w_up, "tp", axis=2, tiled=True)
    down_all = lax.all_gather(w_down, "tp", axis=2, tiled=True)
    gate_act = jnp.einsum("iecd,edf->iecf", received, gate_all, preferred_element_type=jnp.float32)
    up_act = jnp.einsum("iecd,edf->iecf", received, up_all, preferred_element_type=jnp.float32)
    hidden = swiglu(gate_act, up_act).astype(jnp.bfloat16)
    expert_out = jnp.einsum(
        "iecf,edf->iecd", hidden, down_all, preferred_element_type=jnp.float32
    ).astype(jnp.bfloat16)
    returned_output = lax.all_to_all(expert_out, "ep", split_axis=0, concat_axis=0, tiled=True)
    returned_rows = returned_output.reshape(experts * capacity, model_width)
    shard_piece = lax.all_gather(normed, "tp", axis=0, tiled=True)
    gate_act = jnp.dot(shard_piece, shared_gate, preferred_element_type=jnp.float32)
    up_act = jnp.dot(shard_piece, shared_up, preferred_element_type=jnp.float32)
    partial_hidden = swiglu(gate_act, up_act).astype(jnp.bfloat16)
    whole_hidden = lax.all_to_all(partial_hidden, "tp", split_axis=0, concat_axis=1, tiled=True)
    shared_out = jnp.dot(whole_hidden, shared_down, preferred_element_type=jnp.float32)
    safe_target = jnp.where(kept_pair, destination_position, 0)
    picked = jnp.take(returned_rows, safe_target.reshape(-1), axis=0).reshape(
        local_rows, TOP, model_width
    )
    kept_weights = jnp.where(kept_pair, gates, jnp.float32(0.0))
    routed = jnp.sum(picked.astype(jnp.float32) * kept_weights[:, :, None], axis=1)
    return (values + shared_out + routed).astype(jnp.bfloat16)


def solution(mesh):
    placed = (
        P(("ep", "tp"), None),
        P(),
        P(("ep", "tp"), None),
        P(("ep", "tp"), None),
        P(("ep", "tp"), None),
        P(("ep", "tp"), None),
        P("ep", None, "tp"),
        P("ep", None, "tp"),
        P("ep", None, "tp"),
        P(None, "tp"),
        P(None, "tp"),
        P(),
    )
    return jax.shard_map(
        on_device, mesh=mesh, in_specs=placed, out_specs=P(("ep", "tp"), None), check_vma=False
    )
```

profile of v0, /device:TPU:0, one launch (start us, length us, event | category | flops | bytes accessed | tf_op | source)
XLA Modules:
  0.0 298.9 jit_solution(15551164740821854965)
XLA Ops:
  6.5 0.0 copy-start
  6.5 0.0 copy-start.1
  6.5 0.0 copy-start.3
  6.5 0.0 copy-start.6
  6.5 0.0 copy-start.7
  6.6 0.0 all-gather.9.cloned.1.call-start
  6.6 0.7 all-gather.9.cloned.1.call-update
  7.3 0.0 all-gather.11.cloned.1.call-start
  7.3 0.7 all-gather.11.cloned.1.call-update
  8.0 0.0 all-gather.7.cloned.1.call-start
  8.1 0.7 all-gather.7.cloned.1.call-update
  8.8 0.0 copy-done.1
  8.8 0.2 fusion.29
  9.0 0.0 copy-done.3
  9.0 0.2 fusion.31
  9.2 0.0 copy-start.2
  9.2 0.0 copy-done.6
  9.2 0.0 copy-done.5
  9.2 0.0 copy-done.7
  9.3 0.6 fusion.15
  9.9 1.3 convolution_convert_fusion
  11.2 100.4 %all_to_all.29 = bf16[8,2,64,2048]{3,2,1,0:T(8,128)(2,1)} all-to-all(bf16[8,2,64,2048]{3,2,1,0:T(8,128)(2,1)S(1)} %bitcast.62), channel_id=1, replica_groups=mesh['ep'=8,'tp'=4] {'ep'}, dimensions={0} | all-to-all | bytes 8388608 | tf_op jit(solution)/shard_map/all_to_all | solution.py:49
  111.5 0.0 copy-done.2
  111.5 9.2 %fusion.2 = f32[2,8,64,704]{3,2,1,0:T(8,128)} fusion(bf16[2,2048,704]{1,2,0:T(8,128)(2,1)} %all-gather.9.cloned.1.call-done, bf16[8,2,64,2048]{3,2,1,0:T(8,128)(2,1)} %all_to_all.29), kind=kOutput, calls=%fused_computation.4 | convolution fusion | flops 2952790016 | bytes 12845056 | tf_op jit(solution)/shard_map/iecd,edf->iecf/dot_general | solution.py:54
  120.7 24.3 %all-gather.7.cloned.1.call-done = bf16[2,2048,704]{1,2,0:T(8,128)(2,1)} async-done(((bf16[2,2048,176]{1,2,0:T(8,128)(2,1)}), bf16[2,2048,704]{1,2,0:T(8,128)(2,1)}) %all-gather.7.cloned.1.call-update) | async-done | bytes 5767184 | tf_op jit(solution)/shard_map/all_gather | solution.py:50
  145.0 13.1 %convert_bitcast_fusion = bf16[8,2,64,2048]{3,2,0,1:T(8,128)(2,1)} fusion(bf16[2,2048,704]{1,2,0:T(8,128)(2,1)} %all-gather.11.cloned.1.call-done, f32[2,8,64,704]{3,2,1,0:T(8,128)} %fusion.2, bf16[2,2048,704]{1,2,0:T(8,128)(2,1)} %all-gather.7.cloned.1.call-done, bf16[8,2,64,2048]{3,2,1,0:T(8,128)(2,1)} %all_to_all.29), kind=kOutput, calls=%fused_computation.8 | convolution fusion | flops 5912002560 | bytes 22806528 | tf_op jit(solution)/shard_map/iecf,edf->iecd/dot_general | solution.py:56
  158.1 4.7 %copy.39 = bf16[8,2,64,2048]{3,2,1,0:T(8,128)(2,1)} copy(bf16[8,2,64,2048]{3,2,0,1:T(8,128)(2,1)} %convert_bitcast_fusion) | data formatting | bytes 8388608 | tf_op jit(solution)/shard_map/convert_element_type | solution.py:58
  162.9 5.6 %all-to-all-start.2 = ((bf16[8,2,64,2048]{3,2,1,0:T(8,128)(2,1)}), bf16[8,2,64,2048]{3,2,1,0:T(8,128)(2,1)}, u32[]{:S(2)}, u32[]{:S(2)}) async-start(bf16[8,2,64,2048]{3,2,1,0:T(8,128)(2,1)} %copy.39), calls=%async_computation.2 | async-start | bytes 8388608 | tf_op jit(solution)/shard_map/all_to_all | solution.py:59
  168.5 0.0 all-gather.5.cloned.1.call-start
  168.6 0.5 all-gather.5.cloned.1.call-update
  169.1 0.1 copy.40
  169.2 0.1 reshape.66
  169.4 0.0 copy-done.4
  169.4 0.1 copy.41
  169.5 0.1 copy.36
  169.7 24.0 %all-gather.5.cloned.1.call-done = bf16[512,2048]{1,0:T(8,128)(2,1)} async-done(((bf16[128,2048]{1,0:T(8,128)(2,1)}), bf16[512,2048]{1,0:T(8,128)(2,1)}) %all-gather.5.cloned.1.call-update) | async-done | bytes 2097168 | tf_op jit(solution)/shard_map/all_gather | solution.py:61
  193.7 0.0 copy-done
  193.7 2.7 fusion.34
  196.4 0.0 copy-done.8
  196.4 2.4 fusion.28
  198.8 0.8 copy.55
  199.6 62.6 %all-to-all-done.2 = bf16[8,2,64,2048]{3,2,1,0:T(8,128)(2,1)} async-done(((bf16[8,2,64,2048]{3,2,1,0:T(8,128)(2,1)}), bf16[8,2,64,2048]{3,2,1,0:T(8,128)(2,1)}, u32[]{:S(2)}, u32[]{:S(2)}) %all-to-all-start.2) | async-done | bytes 4194336 | tf_op jit(solution)/shard_map/all_to_all | solution.py:59
  262.2 3.6 %all-to-all-start = ((bf16[4,128,352]{1,2,0:T(8,128)(2,1)}), bf16[4,128,352]{1,2,0:T(8,128)(2,1)S(1)}, u32[]{:S(2)}, u32[]{:S(2)}) async-start(bf16[4,128,352]{1,2,0:T(8,128)(2,1)} %bitcast.61), calls=%async_computation | async-start | bytes 720896 | tf_op jit(solution)/shard_map/all_to_all | solution.py:65
  265.9 9.9 %gather_fusion = bf16[768,2048]{1,0:T(8,128)(2,1)} fusion(bf16[1024,2048]{1,0:T(8,128)(2,1)} %bitcast.12, s32[1024]{0:T(1024)S(1)} %pad_clamp_fusion), kind=kCustom, calls=%fused_computation | custom fusion | bytes 6294528 | tf_op jit(solution)/shard_map/jit(_take)/gather | solution.py:68
  275.7 6.2 %gather.7 = bf16[128,6,2048]{2,1,0:T(8,128)(2,1)} reshape(bf16[768,2048]{1,0:T(8,128)(2,1)} %gather_fusion) | data formatting | bytes 6291456 | tf_op jit(solution)/shard_map/jit(_take)/gather | solution.py:68
  282.0 6.0 %multiply_reduce_fusion = f32[128,2048]{1,0:T(8,128)S(1)} fusion(f32[128,6]{1,0:T(8,128)S(1)} %copy.41, bf16[128,6,2048]{2,1,0:T(8,128)(2,1)} %gather.7, pred[128,6]{1,0:T(8,128)(4,1)S(1)} %copy.36), kind=kLoop, calls=%fused_computation.1 | loop fusion | flops 6029312 | bytes 4198144 | tf_op jit(solution)/shard_map/reduce_sum | solution.py:72
  287.9 0.0 all-to-all-done
  287.9 4.4 %fusion.17 = bf16[128,2048]{1,0:T(8,128)(2,1)} fusion(f32[128,2048]{1,0:T(8,128)S(1)} %multiply_reduce_fusion, bf16[128,1408]{0,1:T(8,128)(2,1)S(1)} %bitcast.63, bf16[1408,2048]{1,0:T(8,128)(2,1)} %param.23, bf16[128,2048]{1,0:T(8,128)(2,1)S(1)} %copy-done.1), kind=kOutput, calls=%fused_computation.24 | convolution fusion | flops 739246080 | bytes 8224768 | tf_op jit(solution)/shard_map/dot_general | solution.py:66
  (10 shorter events, 0.1 us)
Async XLA Ops:
  6.5 187.1 %copy-start = (bf16[2048,352]{0,1:T(8,128)(2,1)S(1)}, bf16[2048,352]{0,1:T(8,128)(2,1)}, u32[]{:S(2)}) copy-start(bf16[2048,352]{0,1:T(8,128)(2,1)} %param.21) | copy-start | bytes 4325380
  6.5 2.2 copy-start.1
  6.5 2.4 copy-start.3
  6.5 2.7 copy-start.6
  6.5 2.7 copy-start.5
  6.5 2.7 copy-start.7
  6.6 105.0 %all-gather.9.cloned.1.call-start = ((), (), s32[]{:S(2)}) async-start(), calls=%async_computation.5 | async-start | bytes 7208960 | tf_op jit(solution)/shard_map/all_gather | solution.py:51
  7.3 113.4 %all-gather.11.cloned.1.call-start = ((), (), s32[]{:S(2)}) async-start(), calls=%async_computation.6 | async-start | bytes 7208960 | tf_op jit(solution)/shard_map/all_gather | solution.py:52
  8.0 137.0 %all-gather.7.cloned.1.call-start = ((), (), s32[]{:S(2)}) async-start(), calls=%async_computation.4 | async-start | bytes 7208960 | tf_op jit(solution)/shard_map/all_gather | solution.py:50
  9.2 102.4 %copy-start.2 = (bf16[128,2048]{1,0:T(8,128)(2,1)}, bf16[128,2048]{1,0:T(8,128)(2,1)S(1)}, u32[]{:S(2)}) copy-start(bf16[128,2048]{1,0:T(8,128)(2,1)S(1)} %fusion.31) | copy-start | bytes 1572868
  162.9 6.5 %copy-start.4 = (f32[128,6]{0,1:T(8,128)S(1)}, f32[128,6]{0,1:T(8,128)}, u32[]{:S(2)}) copy-start(f32[128,6]{0,1:T(8,128)} %param.17) | copy-start | bytes 9220
  162.9 99.3 %all-to-all-start.2 = ((bf16[8,2,64,2048]{3,2,1,0:T(8,128)(2,1)}), bf16[8,2,64,2048]{3,2,1,0:T(8,128)(2,1)}, u32[]{:S(2)}, u32[]{:S(2)}) async-start(bf16[8,2,64,2048]{3,2,1,0:T(8,128)(2,1)} %copy.39), calls=%async_computation.2 | async-start | bytes 8388608 | tf_op jit(solution)/shard_map/all_to_all | solution.py:59
  168.5 25.1 %all-gather.5.cloned.1.call-start = ((), (), s32[]{:S(2)}) async-start(), calls=%async_computation.3 | async-start | bytes 2621440 | tf_op jit(solution)/shard_map/all_gather | solution.py:61
  193.7 2.7 copy-start.8
  262.2 25.7 %all-to-all-start = ((bf16[4,128,352]{1,2,0:T(8,128)(2,1)}), bf16[4,128,352]{1,2,0:T(8,128)(2,1)S(1)}, u32[]{:S(2)}, u32[]{:S(2)}) async-start(bf16[4,128,352]{1,2,0:T(8,128)(2,1)} %bitcast.61), calls=%async_computation | async-start | bytes 720896 | tf_op jit(solution)/shard_map/all_to_all | solution.py:65
Sparse Core Ops, SparseCore 0:
  8.9 46.0 all-gather.8
  56.6 43.3 all-gather.10
  101.6 43.3 all-gather.6
  170.6 23.0 all-gather.4
where the time goes:
time: 300 us; the launch traced here: 299 us
  waiting for transfers between devices  114 us (38%)
  blocking collectives  100 us (33%)
  matrix products  33.2 us (11%)
  local copies, waits for them, and re-layouts  22.2 us (7%)
  between operations  13.3 us (4%)
  starting transfers between devices  9.44 us (3%)
  other arithmetic  6.97 us (2%)
    all_to_all x1, blocking collectives, on_device(): lax.all_to_all(boxes, 'ep', split_axis=0, concat_axis=0, tiled=True)  100 us
    all_to_all x1, waiting for transfers between devices, on_device(): lax.all_to_all(expert_out, 'ep', split_axis=0, concat_axis=0, tiled=True)  62.6 us
    all_gather x1, waiting for transfers between devices, on_device(): gate_all = lax.all_gather(w_gate, 'tp', axis=2, tiled=True)  24.3 us
    all_gather x1, waiting for transfers between devices, on_device(): shard_piece = lax.all_gather(normed, 'tp', axis=0, tiled=True)  24 us
    gather x2, local copies, waits for them, and re-layouts, on_device(): jnp.take(returned_rows, safe_target.reshape(-1), axis=0)  16.1 us
    dot_general x1, matrix products, on_device(): jnp.einsum('iecf,edf->iecd', hidden, down_all, preferred_element_type=jnp...  13.1 us
    dot_general x1, matrix products, on_device(): jnp.einsum('iecd,edf->iecf', received, up_all, preferred_element_type=jnp...  9.17 us
  transfers between devices with their start and end apart: 6, of which 3 were waited for; matrix products, arithmetic and copies ran while one was open for 13% of the time, Pallas kernels for 0%

commit v1 on v0

--- a/solution.py
+++ b/solution.py
@@ -7,6 +7,30 @@
 EXP_DEV = 2
 TOK_DEV = 128
 norm_eps = 1e-06
+
+
+def work_both_ways(value, axis, dim, work, out_dim):
+    count, index, extent = (lax.axis_size(axis), lax.axis_index(axis), value.shape[dim])
+    right = [(i, (i + 1) % count) for i in range(count)]
+    left = [(b, a) for a, b in right]
+    lower, upper = (lax.ppermute(value, axis, right), lax.ppermute(value, axis, left))
+    made = work(value, index * extent)
+    length = made.shape[out_dim]
+    out = jnp.zeros((*made.shape[:out_dim], count * length, *made.shape[out_dim + 1 :]), made.dtype)
+
+    def put(out, made, owner):
+        return lax.dynamic_update_slice_in_dim(out, made, owner * length, axis=out_dim)
+
+    out = put(out, made, index)
+    for step in range(1, count // 2 + 1):
+        below, above = ((index - step) % count, (index + step) % count)
+        carried = (lower, upper)
+        if step < count // 2:
+            lower, upper = (lax.ppermute(lower, axis, right), lax.ppermute(upper, axis, left))
+        out = put(out, work(carried[0], below * extent), below)
+        if 2 * step < count:
+            out = put(out, work(carried[1], above * extent), above)
+    return out
 
 
 def swiglu(left, right):
@@ -47,10 +71,17 @@
     ).astype(jnp.bfloat16)
     boxes = outgoing.reshape(n_expert_groups, EXP_DEV, capacity, model_width)
     received = lax.all_to_all(boxes, "ep", split_axis=0, concat_axis=0, tiled=True)
-    gate_all = lax.all_gather(w_gate, "tp", axis=2, tiled=True)
     up_all = lax.all_gather(w_up, "tp", axis=2, tiled=True)
     down_all = lax.all_gather(w_down, "tp", axis=2, tiled=True)
-    gate_act = jnp.einsum("iecd,edf->iecf", received, gate_all, preferred_element_type=jnp.float32)
+    gate_act = work_both_ways(
+        w_gate,
+        "tp",
+        2,
+        lambda own_block, start: jnp.einsum(
+            "iecd,edf->iecf", received, own_block, preferred_element_type=jnp.float32
+        ),
+        3,
+    )
     up_act = jnp.einsum("iecd,edf->iecf", received, up_all, preferred_element_type=jnp.float32)
     hidden = swiglu(gate_act, up_act).astype(jnp.bfloat16)
     expert_out = jnp.einsum(

time: 300 us -> 312 us (1.040)
  blocking collectives: 100 us -> 0 us
  waiting for transfers between devices: 114 us -> 178 us
  local copies, waits for them, and re-layouts: 22.2 us -> 51.2 us
  matrix products: 33.2 us -> 41.5 us
  starting transfers between devices: 9.44 us -> 17.6 us
    all_to_all x1 -> x0, blocking collectives: 100 us -> none  [on_device(): lax.all_to_all(boxes, 'ep', split_axis=0, concat_axis=0, tiled=True)]
    ppermute x0 -> x3, waiting for transfers between devices: none -> 59.6 us  [the longest x1 59.6 us: work_both_ways(): lax.ppermute(value, axis, right)]
    all_to_all x0 -> x1, waiting for transfers between devices: none -> 31.1 us  [on_device(): lax.all_to_all(boxes, 'ep', split_axis=0, concat_axis=0, tiled=True)]
    dynamic_update_slice x0 -> x4, local copies, waits for them, and re-layouts: none -> 27 us  [put(): lax.dynamic_update_slice_in_dim(out, made, owner * length, axis=out_dim)]
    all_gather x1 -> x0, waiting for transfers between devices: 24.3 us -> none  [on_device(): gate_all = lax.all_gather(w_gate, 'tp', axis=2, tiled=True)]
    all_to_all x0 -> x1, starting transfers between devices: none -> 7.31 us  [on_device(): lax.all_to_all(boxes, 'ep', split_axis=0, concat_axis=0, tiled=True)]
    dot_general x1 -> x4, matrix products: 9.17 us -> 15.6 us  [on_device(): jnp.einsum('iecd,edf->iecf', received, own_block, preferred_element_type=...]
  transfers between devices with their start and end apart: 6 -> 9, of which waited for: 3 -> 4; matrix products, arithmetic and copies ran while one was open for 13% -> 26% of each run, Pallas kernels for 0% -> 0%
where the time goes in v1:
time: 312 us; the launch traced here: 311 us
  waiting for transfers between devices  178 us (57%)
  local copies, waits for them, and re-layouts  51.2 us (16%)
  matrix products  41.5 us (13%)
  starting transfers between devices  17.6 us (6%)
  between operations  13.3 us (4%)
  other arithmetic  9.82 us (3%)
    all_to_all x1, waiting for transfers between devices, on_device(): lax.all_to_all(expert_out, 'ep', split_axis=0, concat_axis=0, tiled=True)  60.3 us
    ppermute x1, waiting for transfers between devices, work_both_ways(): lax.ppermute(value, axis, right)  59.6 us
    all_to_all x1, waiting for transfers between devices, on_device(): lax.all_to_all(boxes, 'ep', split_axis=0, concat_axis=0, tiled=True)  31.1 us
    dynamic_update_slice x4, local copies, waits for them, and re-layouts, put(): lax.dynamic_update_slice_in_dim(out, made, owner * length, axis=out_dim)  27 us
    all_gather x1, waiting for transfers between devices, on_device(): shard_piece = lax.all_gather(normed, 'tp', axis=0, tiled=True)  25 us
    gather x2, local copies, waits for them, and re-layouts, on_device(): jnp.take(returned_rows, safe_target.reshape(-1), axis=0)  16.1 us
    dot_general x4, matrix products, on_device(): jnp.einsum('iecd,edf->iecf', received, own_block, preferred_element_type=...  15.6 us
    dot_general x1, matrix products, on_device(): jnp.einsum('iecf,edf->iecd', hidden, down_all, preferred_element_type=jnp...  13.1 us
  transfers between devices with their start and end apart: 9, of which 4 were waited for; matrix products, arithmetic and copies ran while one was open for 26% of the time, Pallas kernels for 0%

profile of v1, /device:TPU:0, one launch (start us, length us, event | category | flops | bytes accessed | tf_op | source)
XLA Modules:
  0.0 311.2 jit_solution(2098325018047507510)
XLA Ops:
  6.5 0.0 all-gather.6.cloned.1.call-start
  6.5 0.7 all-gather.6.cloned.1.call-update
  7.3 1.2 fusion.55
  8.5 0.7 compare_and_fusion
  9.2 0.6 fusion.8
  9.8 1.2 fusion.57
  11.1 0.0 copy-start.2
  11.1 3.2 %convolution_convert_fusion = bf16[1024,2048]{1,0:T(8,128)(2,1)} fusion(pred[128,1024]{1,0:T(8,128)(4,1)S(1)} %fusion.8, bf16[128,2048]{1,0:T(8,128)(2,1)S(1)} %fusion.57), kind=kOutput, calls=%fused_computation.7 | convolution fusion | flops 538968064 | bytes 4849664 | tf_op jit(solution)/shard_map/dot_general | solution.py:69
  14.3 7.3 %all-to-all-start.1 = ((bf16[8,2,64,2048]{3,2,1,0:T(8,128)(2,1)}), bf16[8,2,64,2048]{3,2,1,0:T(8,128)(2,1)}, u32[]{:S(2)}, u32[]{:S(2)}) async-start(bf16[8,2,64,2048]{3,2,1,0:T(8,128)(2,1)} %bitcast.78), calls=%async_computation.1 | async-start | bytes 8388608 | tf_op jit(solution)/shard_map/all_to_all | solution.py:73
  21.6 0.0 all-gather.8.cloned.1.call-start
  21.7 0.7 all-gather.8.cloned.1.call-update
  22.4 0.1 collective-permute-start
  22.5 1.7 collective-permute-start.1
  24.2 59.6 %collective-permute-done = bf16[2,2048,176]{1,2,0:T(8,128)(2,1)} collective-permute-done((bf16[2,2048,176]{1,2,0:T(8,128)(2,1)}, bf16[2,2048,176]{1,2,0:T(8,128)(2,1)}, u32[]{:S(2)}, u32[]{:S(2)}) %collective-permute-start) | collective-permute-done | bytes 1441824 | tf_op jit(solution)/shard_map/ppermute | solution.py:16
  83.8 0.0 collective-permute-start.2
  83.8 31.1 %all-to-all-done.1 = bf16[8,2,64,2048]{3,2,1,0:T(8,128)(2,1)} async-done(((bf16[8,2,64,2048]{3,2,1,0:T(8,128)(2,1)}), bf16[8,2,64,2048]{3,2,1,0:T(8,128)(2,1)}, u32[]{:S(2)}, u32[]{:S(2)}) %all-to-all-start.1) | async-done | bytes 4194336 | tf_op jit(solution)/shard_map/all_to_all | solution.py:73
  114.9 3.9 %fusion.33 = f32[8,2,64,176]{3,2,0,1:T(8,128)S(1)} fusion(bf16[2,2048,176]{1,2,0:T(8,128)(2,1)} %param.18, bf16[8,2,64,2048]{3,2,1,0:T(8,128)(2,1)} %all-to-all-done.1), kind=kOutput, calls=%fused_computation.32 | convolution fusion | flops 738197504 | bytes 6356992 | tf_op jit(solution)/shard_map/iecd,edf->iecf/dot_general | solution.py:80
  118.8 2.0 broadcast_in_dim.26
  120.8 5.8 %dynamic_update_slice.12 = f32[8,2,64,704]{3,2,0,1:T(8,128)} dynamic-update-slice(f32[8,2,64,704]{3,2,0,1:T(8,128)} %broadcast_in_dim.26, f32[8,2,64,176]{3,2,0,1:T(8,128)S(1)} %fusion.33, s32[]{:T(128)} %constant.56.clone.1, s32[]{:T(128)} %constant.56.clone.1, s32[]{:T(128)} %constant.56.clone.1, s32[]{:T(128)S(6)} %select_n.59) | dynamic-update-slice | bytes 1441796 | tf_op jit(solution)/shard_map/dynamic_update_slice | solution.py:22
  126.7 3.9 %fusion.38 = f32[8,2,64,176]{3,2,0,1:T(8,128)S(1)} fusion(bf16[2,2048,176]{1,2,0:T(8,128)(2,1)} %collective-permute-done, bf16[8,2,64,2048]{3,2,1,0:T(8,128)(2,1)} %all-to-all-done.1), kind=kOutput, calls=%fused_computation.33 | convolution fusion | flops 738197504 | bytes 6356992 | tf_op jit(solution)/shard_map/iecd,edf->iecf/dot_general | solution.py:80
  130.6 6.6 %dynamic_update_slice.13 = f32[8,2,64,704]{3,2,0,1:T(8,128)} dynamic-update-slice(f32[8,2,64,704]{3,2,0,1:T(8,128)} %dynamic_update_slice.12, f32[8,2,64,176]{3,2,0,1:T(8,128)S(1)} %fusion.38, s32[]{:T(128)} %constant.56.clone.1, s32[]{:T(128)} %constant.56.clone.1, s32[]{:T(128)} %constant.56.clone.1, s32[]{:T(128)S(6)} %select_n.61) | dynamic-update-slice | bytes 1441796 | tf_op jit(solution)/shard_map/dynamic_update_slice | solution.py:22
  137.2 0.0 collective-permute-done.1
  137.2 3.9 %fusion.43 = f32[8,2,64,176]{3,2,0,1:T(8,128)S(1)} fusion(bf16[2,2048,176]{1,2,0:T(8,128)(2,1)} %collective-permute-done.1, bf16[8,2,64,2048]{3,2,1,0:T(8,128)(2,1)} %all-to-all-done.1), kind=kOutput, calls=%fused_computation.34 | convolution fusion | flops 738197504 | bytes 6356992 | tf_op jit(solution)/shard_map/iecd,edf->iecf/dot_general | solution.py:80
  141.1 7.3 %dynamic_update_slice.14 = f32[8,2,64,704]{3,2,0,1:T(8,128)} dynamic-update-slice(f32[8,2,64,704]{3,2,0,1:T(8,128)} %dynamic_update_slice.13, f32[8,2,64,176]{3,2,0,1:T(8,128)S(1)} %fusion.43, s32[]{:T(128)} %constant.56.clone.1, s32[]{:T(128)} %constant.56.clone.1, s32[]{:T(128)} %constant.56.clone.1, s32[]{:T(128)S(6)} %select_n.63) | dynamic-update-slice | bytes 1441796 | tf_op jit(solution)/shard_map/dynamic_update_slice | solution.py:22
  148.4 0.0 collective-permute-done.2
  148.4 3.9 %fusion.48 = f32[8,2,64,176]{3,2,0,1:T(8,128)S(1)} fusion(bf16[2,2048,176]{1,2,0:T(8,128)(2,1)} %collective-permute-done.2, bf16[8,2,64,2048]{3,2,1,0:T(8,128)(2,1)} %all-to-all-done.1), kind=kOutput, calls=%fused_computation.35 | convolution fusion | flops 738197504 | bytes 6356992 | tf_op jit(solution)/shard_map/iecd,edf->iecf/dot_general | solution.py:80
  152.3 7.3 %dynamic_update_slice.15 = f32[8,2,64,704]{3,2,0,1:T(8,128)} dynamic-update-slice(f32[8,2,64,704]{3,2,0,1:T(8,128)} %dynamic_update_slice.14, f32[8,2,64,176]{3,2,0,1:T(8,128)S(1)} %fusion.48, s32[]{:T(128)} %constant.56.clone.1, s32[]{:T(128)} %constant.56.clone.1, s32[]{:T(128)} %constant.56.clone.1, s32[]{:T(128)S(6)} %select_n.65) | dynamic-update-slice | bytes 1441796 | tf_op jit(solution)/shard_map/dynamic_update_slice | solution.py:22
  159.6 13.1 %convert_bitcast_fusion = bf16[8,2,64,2048]{3,2,0,1:T(8,128)(2,1)} fusion(bf16[2,2048,704]{1,2,0:T(8,128)(2,1)} %all-gather.8.cloned.1.call-done, f32[8,2,64,704]{3,2,0,1:T(8,128)} %dynamic_update_slice.15, bf16[2,2048,704]{1,2,0:T(8,128)(2,1)} %all-gather.6.cloned.1.call-done, bf16[8,2,64,2048]{3,2,1,0:T(8,128)(2,1)} %all-to-all-done.1), kind=kOutput, calls=%fused_computation.6 | convolution fusion | flops 5912002560 | bytes 22806528 | tf_op jit(solution)/shard_map/iecf,edf->iecd/dot_general | solution.py:87
  172.7 4.7 %copy.45 = bf16[8,2,64,2048]{3,2,1,0:T(8,128)(2,1)} copy(bf16[8,2,64,2048]{3,2,0,1:T(8,128)(2,1)} %convert_bitcast_fusion) | data formatting | bytes 8388608 | tf_op jit(solution)/shard_map/convert_element_type | solution.py:89
  177.4 4.7 %all-to-all-start.2 = ((bf16[8,2,64,2048]{3,2,1,0:T(8,128)(2,1)}), bf16[8,2,64,2048]{3,2,1,0:T(8,128)(2,1)}, u32[]{:S(2)}, u32[]{:S(2)}) async-start(bf16[8,2,64,2048]{3,2,1,0:T(8,128)(2,1)} %copy.45), calls=%async_computation.2 | async-start | bytes 8388608 | tf_op jit(solution)/shard_map/all_to_all | solution.py:90
  182.1 0.3 all-gather.4.cloned.1.call-start
  182.4 0.5 all-gather.4.cloned.1.call-update
  182.8 0.1 copy.46
  182.9 0.1 reshape.66
  183.1 0.1 copy.47
  183.2 0.1 copy.39
  183.4 25.0 %all-gather.4.cloned.1.call-done = bf16[512,2048]{1,0:T(8,128)(2,1)} async-done(((bf16[128,2048]{1,0:T(8,128)(2,1)}), bf16[512,2048]{1,0:T(8,128)(2,1)}) %all-gather.4.cloned.1.call-update) | async-done | bytes 2097168 | tf_op jit(solution)/shard_map/all_gather | solution.py:92
  208.4 2.7 fusion.60
  211.1 0.0 copy-done.4
  211.1 2.4 fusion.54
  213.6 0.8 copy.78
  214.4 60.3 %all-to-all-done.2 = bf16[8,2,64,2048]{3,2,1,0:T(8,128)(2,1)} async-done(((bf16[8,2,64,2048]{3,2,1,0:T(8,128)(2,1)}), bf16[8,2,64,2048]{3,2,1,0:T(8,128)(2,1)}, u32[]{:S(2)}, u32[]{:S(2)}) %all-to-all-start.2) | async-done | bytes 4194336 | tf_op jit(solution)/shard_map/all_to_all | solution.py:90
  274.6 3.5 %all-to-all-start = ((bf16[4,128,352]{1,2,0:T(8,128)(2,1)}), bf16[4,128,352]{1,2,0:T(8,128)(2,1)S(1)}, u32[]{:S(2)}, u32[]{:S(2)}) async-start(bf16[4,128,352]{1,2,0:T(8,128)(2,1)} %bitcast.77), calls=%async_computation | async-start | bytes 720896 | tf_op jit(solution)/shard_map/all_to_all | solution.py:96
  278.1 9.8 %gather_fusion = bf16[768,2048]{1,0:T(8,128)(2,1)} fusion(bf16[1024,2048]{1,0:T(8,128)(2,1)} %bitcast.21, s32[1024]{0:T(1024)S(1)} %pad_clamp_fusion), kind=kCustom, calls=%fused_computation | custom fusion | bytes 6294528 | tf_op jit(solution)/shard_map/jit(_take)/gather | solution.py:99
  287.9 6.2 %gather.7 = bf16[128,6,2048]{2,1,0:T(8,128)(2,1)} reshape(bf16[768,2048]{1,0:T(8,128)(2,1)} %gather_fusion) | data formatting | bytes 6291456 | tf_op jit(solution)/shard_map/jit(_take)/gather | solution.py:99
  294.2 6.0 %multiply_reduce_fusion = f32[128,2048]{1,0:T(8,128)S(1)} fusion(f32[128,6]{1,0:T(8,128)S(1)} %copy.47, bf16[128,6,2048]{2,1,0:T(8,128)(2,1)} %gather.7, pred[128,6]{1,0:T(8,128)(4,1)S(1)} %copy.39), kind=kLoop, calls=%fused_computation.1 | loop fusion | flops 6029312 | bytes 4198144 | tf_op jit(solution)/shard_map/reduce_sum | solution.py:103
  300.2 0.0 all-to-all-done
  300.2 4.4 %fusion.10 = bf16[128,2048]{1,0:T(8,128)(2,1)} fusion(f32[128,2048]{1,0:T(8,128)S(1)} %multiply_reduce_fusion, bf16[128,1408]{0,1:T(8,128)(2,1)S(1)} %bitcast.79, bf16[1408,2048]{1,0:T(8,128)(2,1)} %param.23, bf16[128,2048]{1,0:T(8,128)(2,1)S(1)} %copy-done.1), kind=kOutput, calls=%fused_computation.15 | convolution fusion | flops 739246080 | bytes 8224768 | tf_op jit(solution)/shard_map/dot_general | solution.py:97
  (14 shorter events, 0.1 us)
Async XLA Ops:
  6.5 201.9 %copy-start = (bf16[2048,352]{0,1:T(8,128)(2,1)S(1)}, bf16[2048,352]{0,1:T(8,128)(2,1)}, u32[]{:S(2)}) copy-start(bf16[2048,352]{0,1:T(8,128)(2,1)} %param.21) | copy-start | bytes 4325380
  6.5 153.0 %all-gather.6.cloned.1.call-start = ((), (), s32[]{:S(2)}) async-start(), calls=%async_computation.4 | async-start | bytes 7208960 | tf_op jit(solution)/shard_map/all_gather | solution.py:74
  11.1 3.3 %copy-start.2 = (bf16[128,2048]{1,0:T(8,128)(2,1)}, bf16[128,2048]{1,0:T(8,128)(2,1)S(1)}, u32[]{:S(2)}) copy-start(bf16[128,2048]{1,0:T(8,128)(2,1)S(1)} %fusion.57) | copy-start | bytes 1572868
  14.3 100.6 %all-to-all-start.1 = ((bf16[8,2,64,2048]{3,2,1,0:T(8,128)(2,1)}), bf16[8,2,64,2048]{3,2,1,0:T(8,128)(2,1)}, u32[]{:S(2)}, u32[]{:S(2)}) async-start(bf16[8,2,64,2048]{3,2,1,0:T(8,128)(2,1)} %bitcast.78), calls=%async_computation.1 | async-start | bytes 8388608 | tf_op jit(solution)/shard_map/all_to_all | solution.py:73
  21.6 137.9 %all-gather.8.cloned.1.call-start = ((), (), s32[]{:S(2)}) async-start(), calls=%async_computation.5 | async-start | bytes 7208960 | tf_op jit(solution)/shard_map/all_gather | solution.py:75
  22.4 61.4 %collective-permute-start = (bf16[2,2048,176]{1,2,0:T(8,128)(2,1)}, bf16[2,2048,176]{1,2,0:T(8,128)(2,1)}, u32[]{:S(2)}, u32[]{:S(2)}) collective-permute-start(bf16[2,2048,176]{1,2,0:T(8,128)(2,1)} %param.18), channel_id=1, source_target_pairs={{0,1},{1,2},{2,3},{3,0},{4,5},{5,6},{6,7},{7,4},{8,9},{9,10},{10,1... | collective-permute-start | bytes 4325384 | tf_op jit(solution)/shard_map/ppermute | solution.py:16
  22.5 114.7 %collective-permute-start.1 = (bf16[2,2048,176]{1,2,0:T(8,128)(2,1)}, bf16[2,2048,176]{1,2,0:T(8,128)(2,1)}, u32[]{:S(2)}, u32[]{:S(2)}) collective-permute-start(bf16[2,2048,176]{1,2,0:T(8,128)(2,1)} %param.18), channel_id=1, source_target_pairs={{1,0},{2,1},{3,2},{0,3},{5,4},{6,5},{7,6},{4,7},{9,8},{10,9},{11,1... | collective-permute-start | bytes 4325384 | tf_op jit(solution)/shard_map/ppermute | solution.py:16
  83.8 64.6 %collective-permute-start.2 = (bf16[2,2048,176]{1,2,0:T(8,128)(2,1)}, bf16[2,2048,176]{1,2,0:T(8,128)(2,1)}, u32[]{:S(2)}, u32[]{:S(2)}) collective-permute-start(bf16[2,2048,176]{1,2,0:T(8,128)(2,1)} %collective-permute-done), channel_id=1, source_target_pairs={{0,1},{1,2},{2,3},{3,0},{4,5},{5,6},{6,7},{7,4},{8,9},{9,10},{10,1... | collective-permute-start | bytes 4325384 | tf_op jit(solution)/shard_map/ppermute | solution.py:29
  177.4 5.7 %copy-start.3 = (f32[128,6]{0,1:T(8,128)S(1)}, f32[128,6]{0,1:T(8,128)}, u32[]{:S(2)}) copy-start(f32[128,6]{0,1:T(8,128)} %param.17) | copy-start | bytes 9220
  177.4 97.2 %all-to-all-start.2 = ((bf16[8,2,64,2048]{3,2,1,0:T(8,128)(2,1)}), bf16[8,2,64,2048]{3,2,1,0:T(8,128)(2,1)}, u32[]{:S(2)}, u32[]{:S(2)}) async-start(bf16[8,2,64,2048]{3,2,1,0:T(8,128)(2,1)} %copy.45), calls=%async_computation.2 | async-start | bytes 8388608 | tf_op jit(solution)/shard_map/all_to_all | solution.py:90
  182.1 26.3 %all-gather.4.cloned.1.call-start = ((), (), s32[]{:S(2)}) async-start(), calls=%async_computation.3 | async-start | bytes 2621440 | tf_op jit(solution)/shard_map/all_gather | solution.py:92
  208.4 2.7 copy-start.4
  274.6 25.5 %all-to-all-start = ((bf16[4,128,352]{1,2,0:T(8,128)(2,1)}), bf16[4,128,352]{1,2,0:T(8,128)(2,1)S(1)}, u32[]{:S(2)}, u32[]{:S(2)}) async-start(bf16[4,128,352]{1,2,0:T(8,128)(2,1)} %bitcast.77), calls=%async_computation | async-start | bytes 720896 | tf_op jit(solution)/shard_map/all_to_all | solution.py:96
  294.2 6.0 %copy-start.1 = (bf16[128,2048]{1,0:T(8,128)(2,1)S(1)}, bf16[128,2048]{1,0:T(8,128)(2,1)}, u32[]{:S(2)}) copy-start(bf16[128,2048]{1,0:T(8,128)(2,1)} %param.12) | copy-start | bytes 1572868
Sparse Core Ops, SparseCore 0:
  8.9 73.4 all-gather.5
  84.0 51.0 all-gather.7
  184.5 23.9 all-gather.3
